TPU v7x, 32 devices: a whole 2x2x4 slice. The times are simulated.
32 devices in a mesh: blk: 16 (over z, x, core), feat: 2 (over y).
Axes of the slice: x: 2, y: 2, z: 4, core: 2. Of those that a mesh axis runs over, the one named last changes fastest.
Arguments:
- samples: float32 [12288, 2048], P('blk', 'feat'), may hold values from -6 to 6
Outputs:
- band: float32 [5, 12288, 768], P(None, 'blk', 'feat')
All inputs are finite; a program needn't handle non-finite values.
Results may differ from a plain program's by a relative error of at most 0.0001.
Values sent between devices are 32-bit elements; how exact they have to be, the bound alone decides.
A program may use at most 128 MiB of HBM per device.

v0:
```python
import jax
import jax.numpy as jnp
from jax import lax
from jax.sharding import PartitionSpec as P


def from_behind(array, axis, by):
    count = lax.axis_size(axis)
    return lax.ppermute(array, axis, [(i, (i + by) % count) for i in range(count)])


def gram_block(left, right):
    return lax.dot_general(
        left,
        right,
        (((1,), (1,)), ((), ())),
        precision=lax.Precision.HIGHEST,
        preferred_element_type=jnp.float32,
    )


def local(samples):
    width = samples.shape[1] * lax.axis_size("feat")
    scale = 1.0 / jnp.sqrt(jnp.float32(width))
    ahead = [from_behind(samples, "blk", -(step + 1)) for step in range(2)]
    first = gram_block(samples, ahead[0])
    second = gram_block(samples, ahead[1])
    terms = jnp.stack([gram_block(samples, samples), first, second, first.T, second.T])
    summed = lax.psum_scatter(terms * scale, "feat", scatter_dimension=2, tiled=True)
    mirrored = [from_behind(summed[3 + step], "blk", step + 1) for step in range(2)]
    return jnp.stack([mirrored[1], mirrored[0], summed[0], summed[1], summed[2]])


def solution(mesh):
    in_specs = (P("blk", "feat"),)
    out_specs = P(None, "blk", "feat")
    return jax.shard_map(local, mesh=mesh, in_specs=in_specs, out_specs=out_specs, check_vma=False)
```

profile of v0, /device:TPU:1, one launch (start us, length us, event | category | flops | bytes accessed | tf_op | source)
XLA Modules:
  0.0 336.0 jit_solution(5175517363145984868)
XLA Ops:
  6.5 0.0 copy-start
  6.5 0.0 reduce-scatter.2.cloned.1.call-start
  6.5 0.0 collective-permute-start
  6.6 5.7 %collective-permute-start.1 = (f32[768,1024]{1,0:T(8,128)}, f32[768,1024]{1,0:T(8,128)}, u32[]{:S(2)}, u32[]{:S(2)}) collective-permute-start(f32[768,1024]{1,0:T(8,128)} %param.1), channel_id=1, source_target_pairs={{0,28},{2,30},{4,0},{6,2},{8,4},{10,6},{12,8},{14,10},{16,12},{18,... | collective-permute-start | bytes 9437192 | tf_op jit(solution)/shard_map/ppermute | solution.py:9
  12.3 11.9 %bitcast_dynamic-update-slice_fusion.4 = f32[5,768,768]{2,1,0:T(8,128)} fusion(f32[768,1024]{1,0:T(8,128)} %param.1), kind=kOutput, calls=%fused_computation.6 | convolution fusion | flops 7247757312 | bytes 8650752 | tf_op jit(solution)/shard_map/dot_general | solution.py:13
  24.2 53.6 %collective-permute-done = f32[768,1024]{1,0:T(8,128)S(1)} collective-permute-done((f32[768,1024]{1,0:T(8,128)}, f32[768,1024]{1,0:T(8,128)S(1)}, u32[]{:S(2)}, u32[]{:S(2)}) %collective-permute-start) | collective-permute-done | bytes 3145760 | tf_op jit(solution)/shard_map/ppermute | solution.py:9
  77.8 0.0 copy-done
  77.8 9.6 %bitcast_dynamic-update-slice_fusion.3 = (f32[5,768,768]{2,1,0:T(8,128)}, f32[768,768]{1,0:T(8,128)}) fusion(f32[5,768,768]{2,1,0:T(8,128)} %bitcast_dynamic-update-slice_fusion.4, f32[768,1024]{1,0:T(8,128)S(1)} %copy-done, f32[768,1024]{1,0:T(8,128)S(1)} %collective-permute-done), kind=kOutput, calls=%fused_computation.5 | convolution fusion | flops 7247757312 | bytes 11010048 | tf_op jit(solution)/shard_map/dot_general | solution.py:13
  87.4 3.1 copy.2
  90.5 0.0 collective-permute-done.1
  90.5 11.4 %bitcast_dynamic-update-slice_fusion.2 = (f32[5,768,768]{2,1,0:T(8,128)}, f32[768,768]{1,0:T(8,128)}) fusion(f32[5,768,768]{2,1,0:T(8,128)} %get-tuple-element.7, f32[768,1024]{1,0:T(8,128)S(1)} %copy-done, f32[768,1024]{1,0:T(8,128)} %collective-permute-done.1), kind=kOutput, calls=%fused_computation.4 | convolution fusion | flops 7247757312 | bytes 11010048 | tf_op jit(solution)/shard_map/dot_general | solution.py:13
  101.9 0.0 copy-start.1
  101.9 3.2 copy.3
  105.1 0.0 copy-start.2
  105.1 0.0 copy-done.1
  105.1 1.5 bitcast_dynamic-update-slice_fusion.1
  106.7 1.0 copy-done.2
  107.7 1.6 bitcast_dynamic-update-slice_fusion
  109.3 10.0 %broadcast_multiply_fusion = f32[5,768,768]{2,1,0:T(8,128)} fusion(f32[5,768,768]{2,1,0:T(8,128)} %bitcast_dynamic-update-slice_fusion), kind=kLoop, calls=%fused_computation.1 | loop fusion | flops 2949120 | bytes 23592960 | tf_op jit(solution)/shard_map/mul | solution.py:29
  119.3 0.0 reduce-scatter.2.cloned.1.call-update
  119.3 161.3 %reduce-scatter.2.cloned.1.call-done = f32[5,768,384]{2,1,0:T(8,128)} async-done(((f32[5,768,768]{2,1,0:T(8,128)}), f32[5,768,384]{2,1,0:T(8,128)}) %reduce-scatter.2.cloned.1.call-update) | async-done | bytes 5898256 | tf_op jit(solution)/shard_map/reduce_scatter | solution.py:29
  280.6 1.8 slice_bitcast_fusion.1
  282.4 2.0 collective-permute-start.3
  284.3 0.0 slice-start
  284.3 1.2 collective-permute-start.2
  285.6 23.9 %collective-permute-done.3 = f32[768,384]{1,0:T(8,128)S(1)} collective-permute-done((f32[768,384]{1,0:T(8,128)S(1)}, f32[768,384]{1,0:T(8,128)S(1)}, u32[]{:S(2)}, u32[]{:S(2)}) %collective-permute-start.3) | collective-permute-done | bytes 1179680 | tf_op jit(solution)/shard_map/ppermute | solution.py:9
  309.5 16.7 %collective-permute-done.2 = f32[768,384]{1,0:T(8,128)S(1)} collective-permute-done((f32[768,384]{1,0:T(8,128)S(1)}, f32[768,384]{1,0:T(8,128)S(1)}, u32[]{:S(2)}, u32[]{:S(2)}) %collective-permute-start.2) | collective-permute-done | bytes 1179680 | tf_op jit(solution)/shard_map/ppermute | solution.py:9
  326.2 0.0 slice-done
  326.2 3.0 pad_maximum_fusion
Async XLA Ops:
  6.5 71.3 %copy-start = (f32[768,1024]{1,0:T(8,128)S(1)}, f32[768,1024]{1,0:T(8,128)}, u32[]{:S(2)}) copy-start(f32[768,1024]{1,0:T(8,128)} %param.1) | copy-start | bytes 9437188
  6.5 274.1 %reduce-scatter.2.cloned.1.call-start = ((), (), s32[]{:S(2)}) async-start(), calls=%async_computation.1 | async-start | bytes 17694720 | tf_op jit(solution)/shard_map/reduce_scatter | solution.py:29
  6.5 71.3 %collective-permute-start = (f32[768,1024]{1,0:T(8,128)}, f32[768,1024]{1,0:T(8,128)S(1)}, u32[]{:S(2)}, u32[]{:S(2)}) collective-permute-start(f32[768,1024]{1,0:T(8,128)} %param.1), channel_id=1, source_target_pairs={{0,30},{2,0},{4,2},{6,4},{8,6},{10,8},{12,10},{14,12},{16,14},{18,... | collective-permute-start | bytes 9437192 | tf_op jit(solution)/shard_map/ppermute | solution.py:9
  6.6 84.0 %collective-permute-start.1 = (f32[768,1024]{1,0:T(8,128)}, f32[768,1024]{1,0:T(8,128)}, u32[]{:S(2)}, u32[]{:S(2)}) collective-permute-start(f32[768,1024]{1,0:T(8,128)} %param.1), channel_id=1, source_target_pairs={{0,28},{2,30},{4,0},{6,2},{8,4},{10,6},{12,8},{14,10},{16,12},{18,... | collective-permute-start | bytes 9437192 | tf_op jit(solution)/shard_map/ppermute | solution.py:9
  101.9 3.2 copy-start.1
  105.1 2.5 copy-start.2
  282.4 27.1 %collective-permute-start.3 = (f32[768,384]{1,0:T(8,128)S(1)}, f32[768,384]{1,0:T(8,128)S(1)}, u32[]{:S(2)}, u32[]{:S(2)}) collective-permute-start(f32[768,384]{1,0:T(8,128)S(1)} %get-tuple-element.6), channel_id=1, source_target_pairs={{0,2},{2,4},{4,6},{6,8},{8,10},{10,12},{12,14},{14,16},{16,18},{18... | collective-permute-start | bytes 3538952 | tf_op jit(solution)/shard_map/ppermute | solution.py:9
  284.3 41.9 %slice-start = ((f32[5,768,384]{2,1,0:T(8,128)}), f32[3,768,384]{2,1,0:T(8,128)S(1)}, s32[]{:S(2)}) async-start(f32[5,768,384]{2,1,0:T(8,128)} %reduce-scatter.2.cloned.1.call-done), calls=%async_computation.2 | async-start | bytes 7077888 | tf_op jit(solution)/shard_map/slice | solution.py:31
  284.3 41.8 %collective-permute-start.2 = (f32[768,384]{1,0:T(8,128)S(1)}, f32[768,384]{1,0:T(8,128)S(1)}, u32[]{:S(2)}, u32[]{:S(2)}) collective-permute-start(f32[768,384]{1,0:T(8,128)S(1)} %get-tuple-element.5), channel_id=1, source_target_pairs={{0,4},{2,6},{4,8},{6,10},{8,12},{10,14},{12,16},{14,18},{16,20},{1... | collective-permute-start | bytes 3538952 | tf_op jit(solution)/shard_map/ppermute | solution.py:9
Sparse Core Ops, SparseCore 0:
  119.4 161.1 reduce-scatter.1
where the time goes:
time: 336 us
  waiting for transfers between devices  256 us (76%)
  matrix products  32.9 us (10%)
  between operations  13.4 us (4%)
  other arithmetic  13 us (4%)
  local copies, waits for them, and re-layouts  12.2 us (4%)
  starting transfers between devices  8.92 us (3%)
    reduce_scatter x1, waiting for transfers between devices, local(): lax.psum_scatter(terms * scale, 'feat', scatter_dimension=2, tiled=True)  161 us
    ppermute x4, waiting for transfers between devices, from_behind(): lax.ppermute(array, axis, [(i, (i + by) % count) for i in range(count)])  94.2 us
    dot_general x3, matrix products, gram_block(): lax.dot_general(left, right, (((1,), (1,)), ((), ())), precision=lax.Prec...  32.9 us
    mul x1, other arithmetic, local(): terms * scale  10 us
    ppermute x4, starting transfers between devices, from_behind(): lax.ppermute(array, axis, [(i, (i + by) % count) for i in range(count)])  8.92 us
  transfers between devices with their start and end apart: 5, of which 4 were waited for; matrix products, arithmetic and copies ran while one was open for 7% of the time, Pallas kernels for 0%

commit v1 on v0

v1 whole, which is shorter than its diff:
```python
import functools

import jax
import jax.numpy as jnp
from jax import lax
from jax.experimental import pallas as pl
from jax.experimental.pallas import tpu as pltpu
from jax.sharding import PartitionSpec as P

MESH = pl.DeviceIdType.MESH
CHUNK = 128
AHEAD = 3
RING = 3
Y, X, Z, C, R = range(5)


def left_split(value):
    high = value.astype(jnp.bfloat16)
    low = (value - high.astype(jnp.float32)).astype(jnp.bfloat16)
    return jnp.concatenate([high, high, low], axis=1)


def right_split(value):
    high = value.astype(jnp.bfloat16)
    low = (value - high.astype(jnp.float32)).astype(jnp.bfloat16)
    return jnp.concatenate([high, low, high], axis=1)


def kernel(n, scale, x_hbm, o_hbm, own, bx, bz, bc, br, acc, left, send, recv, local, outs):
    rows = x_hbm.shape[0]
    half = rows // 2
    kl = x_hbm.shape[1] // CHUNK
    steps = 2 * kl
    b, f = lax.axis_index("blk"), lax.axis_index("feat")
    core = lax.rem(b, 2)
    group = lax.rem(b // 2, 2)
    near = b + 2 - 4 * group
    onward = lax.rem(b + jnp.where(group == 0, 4, n - 4), n)
    source = lax.rem(b + jnp.where(group == 0, n - 4, 4), n)
    mate = b + 1 - 2 * core
    gives_x = core == group

    def mine(k, h):
        start = pl.multiple_of(jnp.where(h == 0, f, 1 - f) * half, half)
        column = pl.multiple_of(k * CHUNK, CHUNK)
        return pltpu.make_async_copy(
            x_hbm.at[pl.ds(start, half), pl.ds(column, CHUNK)], own.at[k, h], local.at[h, k]
        )

    def remote(kind, k, src, dst, target):
        return pltpu.make_async_remote_copy(
            src_ref=src,
            dst_ref=dst,
            send_sem=send.at[kind, k],
            recv_sem=recv.at[kind, k],
            device_id=target,
            device_id_type=MESH,
        )

    def y_copy(t):
        k, phase = lax.rem(t, kl), t // kl
        return remote(Y, t, own.at[k, 1 - phase], own.at[kl + k, phase], (b, 1 - f))

    def x_copy(k):
        return remote(X, k, own.at[k, 0], bx.at[k], (near, f))

    def z_copy(k):
        return remote(Z, k, bx.at[k], bz.at[k], (onward, f))

    def c_copy(k):
        return remote(C, k, own.at[k, 0], bc.at[k], (mate, f))

    def r_copy(k, src):
        return remote(R, k, src.at[k], br.at[k], (mate, f))

    def load(k, _):
        mine(k, 0).start()
        mine(k, 1).start()
        return 0

    lax.fori_loop(0, kl, load, 0)
    barrier = pltpu.get_barrier_semaphore()
    for device in ((b, 1 - f), (near, f), (mate, f), (onward, f), (source, f)):
        pl.semaphore_signal(barrier, inc=1, device_id=device, device_id_type=MESH)
    pl.semaphore_wait(barrier, 5)

    def begin(k, _):
        mine(k, 0).wait()
        mine(k, 1).wait()

        @pl.when(k < AHEAD)
        def _():
            x_copy(k).start()
            y_copy(k).start()

        c_copy(k).start()
        return 0

    lax.fori_loop(0, kl, begin, 0)
    acc[...] = jnp.zeros_like(acc)

    def add(j, k, block):
        acc[j] += lax.dot_general(
            left[lax.rem(k, RING)],
            right_split(block),
            (((1,), (1,)), ((), ())),
            preferred_element_type=jnp.float32,
        )

    def step(t, _):
        @pl.when(t < steps)
        def _():
            y_copy(t).wait_recv()

            @pl.when(t < kl)
            def _():
                c_copy(kl + t).start()

            @pl.when(t + AHEAD < steps)
            def _():
                x_copy(t + AHEAD).start()
                y_copy(t + AHEAD).start()

            x_copy(t).wait_recv()
            z_copy(t).start()

            @pl.when(gives_x)
            def _():
                r_copy(t, bx).start()

        @pl.when(jnp.logical_and(t >= 1, t <= steps))
        def _():
            z_copy(t - 1).wait_recv()

            @pl.when(jnp.logical_not(gives_x))
            def _():
                r_copy(t - 1, bz).start()

        @pl.when(t < steps)
        def _():
            c_copy(t).wait_recv()
            whole = own[t].reshape(rows, CHUNK)
            left[lax.rem(t, RING)] = left_split(whole * scale)
            add(0, t, own[t, 0])
            add(1, t, bc[t])
            add(2, t, bx[t])

        @pl.when(jnp.logical_and(t >= 1, t <= steps))
        def _():
            add(3, t - 1, bz[t - 1])

        @pl.when(t >= 2)
        def _():
            r_copy(t - 2, bx).wait_recv()
            add(4, t - 2, br[t - 2])

        return 0

    lax.fori_loop(0, steps + 2, step, 0)

    slots = (2, 3 - 2 * core, 4 - 4 * group, 4 * group, 1 + 2 * core)

    def out(j, h):
        start = pl.multiple_of((f if h == 0 else 1 - f) * half, half)
        return pltpu.make_async_copy(
            acc.at[j, pl.ds(h * half, half)], o_hbm.at[slots[j], pl.ds(start, half)], outs.at[j, h]
        )

    for j in range(5):
        for h in range(2):
            out(j, h).start()

    def drain(k, _):
        y_copy(k).wait_send()
        x_copy(k).wait_send()
        z_copy(k).wait_send()
        c_copy(k).wait_send()
        r_copy(k, bx).wait_send()
        return 0

    lax.fori_loop(0, steps, drain, 0)
    for j in range(5):
        for h in range(2):
            out(j, h).wait()


def solution(mesh):
    n = mesh.shape["blk"]

    def local(samples):
        rows, width = samples.shape
        half = rows // 2
        steps = 2 * width // CHUNK
        block = pltpu.VMEM((steps, half, CHUNK), jnp.float32)
        scale = 1.0 / float(width * mesh.shape["feat"]) ** 0.5
        return pl.pallas_call(
            functools.partial(kernel, n, scale),
            out_shape=jax.ShapeDtypeStruct((5, rows, half), jnp.float32),
            in_specs=[pl.BlockSpec(memory_space=pl.ANY)],
            out_specs=pl.BlockSpec(memory_space=pl.ANY),
            scratch_shapes=[
                pltpu.VMEM((steps, 2, half, CHUNK), jnp.float32),
                block,
                block,
                block,
                block,
                pltpu.VMEM((5, rows, half), jnp.float32),
                pltpu.VMEM((RING, rows, 3 * CHUNK), jnp.bfloat16),
                pltpu.SemaphoreType.DMA((5, steps)),
                pltpu.SemaphoreType.DMA((5, steps)),
                pltpu.SemaphoreType.DMA((2, steps // 2)),
                pltpu.SemaphoreType.DMA((5, 2)),
            ],
            compiler_params=pltpu.CompilerParams(
                collective_id=0, has_side_effects=True, vmem_limit_bytes=60 << 20
            ),
            name="band",
        )(samples)

    return jax.shard_map(
        local, mesh=mesh, in_specs=(P("blk", "feat"),), out_specs=P(None, "blk", "feat"), check_vma=False
    )
```

time: 336 us -> 93 us (0.28)
  the two profiles are of different devices: /device:TPU:1 before, /device:TPU:3 now
where the time goes in v1:
time: 93 us; the launch traced here: 92.8 us
  Pallas kernels  87.2 us (94%)
  local copies, waits for them, and re-layouts  5.63 us (6%)
    pallas_call x1, Pallas kernels, local(): pl.pallas_call(functools.partial(kernel, n, scale), out_shape=jax.ShapeDt...  87.2 us
    unnamed x1, local copies, waits for them, and re-layouts  5.63 us

profile of v1, /device:TPU:3, one launch (start us, length us, event | category | flops | bytes accessed | tf_op | source)
XLA Modules:
  0.0 92.8 jit_solution(13962119255446971898)
XLA Ops:
  0.0 87.2 %band.1 = f32[5,768,384]{2,1,0:T(8,128)} custom-call(f32[768,1024]{1,0:T(8,128)} %x_hbm.1), custom_call_target="tpu_custom_call" | custom-call | tf_op jit(solution)/shard_map/band/pallas_call | solution.py:196
  87.2 5.6 %copy.3 = f32[5,768,384]{2,1,0:T(8,128)} copy(f32[5,768,384]{2,1,0:T(8,128)} %band.1) | data formatting | bytes 11796480

commit v2 on v1

v2 whole, which is shorter than its diff:
```python
import functools

import jax
import jax.numpy as jnp
from jax import lax
from jax.experimental import pallas as pl
from jax.experimental.pallas import tpu as pltpu
from jax.sharding import PartitionSpec as P

MESH = pl.DeviceIdType.MESH
CHUNK = 128
PARTS = 1
AHEAD = 3
RING = 3
Y, C, R = range(3)


def left_split(value):
    high = value.astype(jnp.bfloat16)
    low = (value - high.astype(jnp.float32)).astype(jnp.bfloat16)
    return jnp.concatenate([high, high, low], axis=1)


def right_split(value):
    high = value.astype(jnp.bfloat16)
    low = (value - high.astype(jnp.float32)).astype(jnp.bfloat16)
    return jnp.concatenate([high, low, high], axis=1)


def kernel(n, scale, x_hbm, acc, own, bx, bz, bc, br, left, send, recv, sendx, recvx, sendz, recvz, local):
    rows = x_hbm.shape[0]
    half = rows // 2
    kl = x_hbm.shape[1] // CHUNK
    steps = 2 * kl
    b, f = lax.axis_index("blk"), lax.axis_index("feat")
    core = lax.rem(b, 2)
    group = lax.rem(b // 2, 2)
    near = b + 2 - 4 * group
    onward = lax.rem(b + jnp.where(group == 0, 4, n - 4), n)
    source = lax.rem(b + jnp.where(group == 0, n - 4, 4), n)
    mate = b + 1 - 2 * core
    gives_x = core == group

    def mine(k, h):
        start = pl.multiple_of(jnp.where(h == 0, f, 1 - f) * half, half)
        column = pl.multiple_of(k * CHUNK, CHUNK)
        return pltpu.make_async_copy(
            x_hbm.at[pl.ds(start, half), pl.ds(column, CHUNK)], own.at[k, h], local.at[h, k]
        )

    def remote(kind, k, src, dst, target):
        return pltpu.make_async_remote_copy(
            src_ref=src,
            dst_ref=dst,
            send_sem=send.at[kind, k],
            recv_sem=recv.at[kind, k],
            device_id=target,
            device_id_type=MESH,
        )

    def y_copy(t):
        k, phase = lax.rem(t, kl), t // kl
        return remote(Y, t, own.at[k, 1 - phase], own.at[kl + k, phase], (b, 1 - f))

    def part(s):
        return pl.ds(s * (half // PARTS), half // PARTS)

    def x_copy(k, s):
        return pltpu.make_async_remote_copy(
            src_ref=own.at[k, 0, part(s)],
            dst_ref=bx.at[k, part(s)],
            send_sem=sendx.at[s, k],
            recv_sem=recvx.at[s, k],
            device_id=(near, f),
            device_id_type=MESH,
        )

    def z_copy(k, s):
        return pltpu.make_async_remote_copy(
            src_ref=bx.at[k, part(s)],
            dst_ref=bz.at[k, part(s)],
            send_sem=sendz.at[s, k],
            recv_sem=recvz.at[s, k],
            device_id=(onward, f),
            device_id_type=MESH,
        )

    def c_copy(k):
        return remote(C, k, own.at[k, 0], bc.at[k], (mate, f))

    def r_copy(k, src):
        return remote(R, k, src.at[k], br.at[k], (mate, f))

    def load(k, _):
        mine(k, 0).start()
        mine(k, 1).start()
        return 0

    lax.fori_loop(0, kl, load, 0)
    barrier = pltpu.get_barrier_semaphore()
    for device in ((b, 1 - f), (near, f), (mate, f), (onward, f), (source, f)):
        pl.semaphore_signal(barrier, inc=1, device_id=device, device_id_type=MESH)
    pl.semaphore_wait(barrier, 5)

    def begin(k, _):
        mine(k, 0).wait()
        mine(k, 1).wait()

        @pl.when(k < AHEAD)
        def _():
            for s in range(PARTS):
                x_copy(k, s).start()
            y_copy(k).start()

        c_copy(k).start()
        return 0

    lax.fori_loop(0, kl, begin, 0)
    acc[...] = jnp.zeros_like(acc)

    slots = (2, 3 - 2 * core, 4 - 4 * group, 4 * group, 1 + 2 * core)

    def add(j, k, block):
        right = right_split(block)
        for h in range(2):
            start = pl.multiple_of((f if h == 0 else 1 - f) * half, half)
            acc[slots[j], pl.ds(start, half)] += lax.dot_general(
                left[lax.rem(k, RING), h],
                right,
                (((1,), (1,)), ((), ())),
                preferred_element_type=jnp.float32,
            )

    def step(t, _):
        for s in range(PARTS):

            @pl.when(t < steps)
            def _():
                if s == 0:
                    y_copy(t).wait_recv()

                    @pl.when(t < kl)
                    def _():
                        c_copy(kl + t).start()

                    @pl.when(t + AHEAD < steps)
                    def _():
                        for r in range(PARTS):
                            x_copy(t + AHEAD, r).start()
                        y_copy(t + AHEAD).start()

                x_copy(t, s).wait_recv()
                z_copy(t, s).start()

                if s == PARTS - 1:

                    @pl.when(gives_x)
                    def _():
                        r_copy(t, bx).start()

                if s == 0:
                    for h in range(2):
                        left[lax.rem(t, RING), h] = left_split(own[t, h] * scale)
                    add(0, t, own[t, 0])
                if s == PARTS - 1:
                    c_copy(t).wait_recv()
                    add(1, t, bc[t])

            if s == 0:

                @pl.when(jnp.logical_and(t >= 1, t <= steps))
                def _():
                    for r in range(PARTS):
                        z_copy(t - 1, r).wait_recv()

                    @pl.when(jnp.logical_not(gives_x))
                    def _():
                        r_copy(t - 1, bz).start()

                    add(3, t - 1, bz[t - 1])

        @pl.when(t < steps)
        def _():
            add(2, t, bx[t])

        @pl.when(t >= 2)
        def _():
            r_copy(t - 2, bx).wait_recv()
            add(4, t - 2, br[t - 2])

        return 0

    lax.fori_loop(0, steps + 2, step, 0)

    def drain(k, _):
        y_copy(k).wait_send()
        for s in range(PARTS):
            x_copy(k, s).wait_send()
            z_copy(k, s).wait_send()
        c_copy(k).wait_send()
        r_copy(k, bx).wait_send()
        return 0

    lax.fori_loop(0, steps, drain, 0)


def solution(mesh):
    n = mesh.shape["blk"]

    def local(samples):
        rows, width = samples.shape
        half = rows // 2
        steps = 2 * width // CHUNK
        block = pltpu.VMEM((steps, half, CHUNK), jnp.float32)
        scale = 1.0 / float(width * mesh.shape["feat"]) ** 0.5
        return pl.pallas_call(
            functools.partial(kernel, n, scale),
            out_shape=pltpu.VMEM((5, rows, half), jnp.float32),
            in_specs=[pl.BlockSpec(memory_space=pl.ANY)],
            out_specs=pl.BlockSpec(memory_space=pltpu.VMEM),
            scratch_shapes=[
                pltpu.VMEM((steps, 2, half, CHUNK), jnp.float32),
                block,
                block,
                block,
                block,
                pltpu.VMEM((RING, 2, half, 3 * CHUNK), jnp.bfloat16),
                pltpu.SemaphoreType.DMA((3, steps)),
                pltpu.SemaphoreType.DMA((3, steps)),
                pltpu.SemaphoreType.DMA((PARTS, steps)),
                pltpu.SemaphoreType.DMA((PARTS, steps)),
                pltpu.SemaphoreType.DMA((PARTS, steps)),
                pltpu.SemaphoreType.DMA((PARTS, steps)),
                pltpu.SemaphoreType.DMA((2, steps // 2)),
            ],
            compiler_params=pltpu.CompilerParams(
                collective_id=0, has_side_effects=True, vmem_limit_bytes=48 << 20
            ),
            name="band",
        )(samples)

    return jax.shard_map(
        local, mesh=mesh, in_specs=(P("blk", "feat"),), out_specs=P(None, "blk", "feat"), check_vma=False
    )
```

time: 93 us -> 86.9 us (0.934)
  the two profiles are of different devices: /device:TPU:3 before, /device:TPU:1 now
where the time goes in v2:
time: 86.9 us; the launch traced here: 85.4 us
  Pallas kernels  82.8 us (95%)
  local copies, waits for them, and re-layouts  2.58 us (3%)
    pallas_call x1, Pallas kernels, local(): pl.pallas_call(functools.partial(kernel, n, scale), out_shape=pltpu.VMEM(...  82.8 us
    unnamed x1, local copies, waits for them, and re-layouts  2.58 us

profile of v2, /device:TPU:1, one launch (start us, length us, event | category | flops | bytes accessed | tf_op | source)
XLA Modules:
  0.0 85.4 jit_solution(4724682616934824018)
XLA Ops:
  0.0 82.8 %band.1 = f32[5,768,384]{2,1,0:T(8,128)S(1)} custom-call(f32[768,1024]{1,0:T(8,128)} %x_hbm.1), custom_call_target="tpu_custom_call" | custom-call | tf_op jit(solution)/shard_map/band/pallas_call | solution.py:216
  82.8 2.6 %copy.3 = f32[5,768,384]{2,1,0:T(8,128)} copy(f32[5,768,384]{2,1,0:T(8,128)S(1)} %band.1) | data formatting | bytes 11796480
